TPU v7x, 32 devices: a whole 2x2x4 slice. The times are simulated.
32 devices in a mesh: member: 8 (over z, y), region: 4 (over x, core).
Axes of the slice: x: 2, y: 2, z: 4, core: 2. Of those that a mesh axis runs over, the one named last changes fastest.
Arguments:
- ensemble: bfloat16 [512, 32768], P(('member', 'region')), may hold values from -12 to 12
- obs_offset: int32 [4, 8, 16], P('region', 'member'), may hold values from 0 to 1023
- observed: float32 [4, 8, 16], P('region', 'member'), may hold values from -12 to 12
- obs_var: float32 [4, 8, 16], P('region', 'member'), may hold values from 0.2 to 2
Outputs:
- analysis: bfloat16 [512, 32768], P(('member', 'region'))
Inputs may be any that keep to these rules, and one draw needn't show every extreme that they name: obs_offset indexes a link within the block of 1024 links; two detectors may watch the same link.
All inputs are finite; a program needn't handle non-finite values.
Results may differ from a plain program's by a relative error of at most 0.0019.
Values may be sent and summed in bfloat16 or wider, within the bound.
A program may use at most 128 MiB of HBM per device.

v0:
```python
import jax
import jax.numpy as jnp
from jax import lax
from jax.sharding import PartitionSpec as P


def observation_terms(picked, values, variance, ensemble_size):
    center = jnp.mean(picked, axis=1, keepdims=True)
    anomaly = picked - center
    innovation = values - center[:, 0]
    numer = jnp.sum(innovation * innovation)
    denom = jnp.sum(jnp.sum(anomaly * anomaly, axis=1) / (ensemble_size - 1.0) + variance)
    weight = 1.0 / ((ensemble_size - 1.0) * variance)
    return (anomaly, innovation, weight, numer, denom)


def weighted_products(anomaly, innovation, weight):
    weighted = anomaly * weight[:, None]
    products = jnp.dot(weighted.T, anomaly, precision=lax.Precision.HIGHEST)
    column = jnp.dot(innovation * weight, anomaly, precision=lax.Precision.HIGHEST)
    return (products, column)


def mixing_matrix(products, column, lift, diag_coef, col_coef, mat_coef):
    identity = jnp.eye(products.shape[0], dtype=jnp.float32)
    system = identity + lift * products
    factor = jnp.linalg.cholesky(system)
    right_side = jnp.concatenate([products, column[:, None]], axis=1)
    solved = jax.scipy.linalg.cho_solve((factor, True), right_side)
    return diag_coef * identity + col_coef * solved[:, -1][None, :] - mat_coef * solved[:, :-1]


def local(ensemble, obs_offset, observed, obs_var):
    members = lax.axis_size("member")
    regions = lax.axis_size("region")
    own_count = ensemble.shape[0]
    ensemble_size = own_count * members * regions
    link_count = ensemble.shape[1] // (members * regions)
    shifted = lax.all_to_all(
        lax.all_to_all(ensemble, "region", split_axis=1, concat_axis=0, tiled=True),
        "member",
        split_axis=1,
        concat_axis=0,
        tiled=True,
    )
    values = observed.reshape(-1)
    variance = obs_var.reshape(-1)
    region_offsets = lax.all_gather(obs_offset, "member", axis=1, tiled=True)
    every_offset = lax.all_gather(region_offsets, "region", axis=0, tiled=True)
    region_block = lax.broadcasted_iota(jnp.int32, every_offset.shape, 0)
    member_block = lax.broadcasted_iota(jnp.int32, every_offset.shape, 1)
    link_index = ((region_block * members + member_block) * link_count + every_offset).reshape(-1)
    own_rows = jnp.take(ensemble, link_index, axis=1).reshape(own_count, regions, -1)
    local_rows = lax.all_to_all(own_rows, "region", split_axis=1, concat_axis=0, tiled=True)
    local_rows = local_rows.reshape(own_count * regions, -1)
    obs_rows = lax.all_gather(local_rows, "member", axis=0, tiled=True)
    region_values, region_variance = (
        lax.all_gather(values, "member", axis=0, tiled=True),
        lax.all_gather(variance, "member", axis=0, tiled=True),
    )
    picked = obs_rows.T.astype(jnp.float32)
    anomaly, innovation, weight, numer, denom = observation_terms(
        picked, region_values, region_variance, ensemble_size
    )
    numer, denom = lax.psum((numer, denom), "region")
    inflation = jnp.sqrt(numer / denom)
    products, column = weighted_products(inflation * anomaly, innovation, weight)
    products, column = lax.psum((products, column), "region")
    mixing = mixing_matrix(products, column, 1.0, inflation, inflation, 0.5 * inflation)
    state_values = shifted.astype(jnp.float32)
    center = jnp.mean(state_values, axis=0, keepdims=True)
    updated = (
        center + jnp.dot(mixing, state_values - center, precision=lax.Precision.HIGHEST)
    ).astype(jnp.bfloat16)
    return lax.all_to_all(
        lax.all_to_all(updated, "member", split_axis=0, concat_axis=1, tiled=True),
        "region",
        split_axis=0,
        concat_axis=1,
        tiled=True,
    )


def solution(mesh):
    return jax.shard_map(
        local,
        mesh=mesh,
        in_specs=(
            P(("member", "region"), None),
            P("region", "member", None),
            P("region", "member", None),
            P("region", "member", None),
        ),
        out_specs=P(("member", "region"), None),
        check_vma=False,
    )
```

profile of v0, /device:TPU:0, one launch (start us, length us, event | category | flops | bytes accessed | tf_op | source)
XLA Modules:
  0.0 394.2 jit_solution(4288350001859366908)
XLA Ops:
  6.5 22.5 %all_gather.16 = s32[1,8,16]{2,0,1:T(1,128)S(1)} all-gather(s32[1,1,16]{2,0,1:T(1,128)} %bitcast.112), channel_id=1, replica_groups=mesh['member'=8,'region'=4] {'member'}, dimensions={1}, use_global_device_ids=true | all-gather | bytes 576 | tf_op jit(solution)/shard_map/all_gather | solution.py:48
  29.0 5.2 %all_gather.17 = s32[4,8,16]{2,1,0:T(8,128)S(1)} all-gather(s32[1,8,16]{2,1,0:T(8,128)S(1)} %bitcast.109), channel_id=1, replica_groups=mesh['member'=8,'region'=4] {'region'}, dimensions={0}, use_global_device_ids=true | all-gather | bytes 2560 | tf_op jit(solution)/shard_map/all_gather | solution.py:49
  34.5 7.1 %copy.51 = bf16[16,32768]{0,1:T(8,128)(2,1)} copy(bf16[16,32768]{1,0:T(8,128)(2,1)} %param.4) | data formatting | bytes 2097152 | tf_op args[0]
  41.5 5.6 %gather_fusion = bf16[512,16]{1,0:T(8,128)(2,1)S(1)} fusion(bf16[16,32768]{0,1:T(8,128)(2,1)} %copy.51, s32[1024]{0:T(1024)S(1)} %pad_clamp_fusion), kind=kCustom, calls=%fused_computation | custom fusion | bytes 34816 | tf_op jit(solution)/shard_map/jit(_take)/gather | solution.py:53
  47.9 3.3 all-to-all-start.2
  51.2 0.7 dynamic-slice.3
  52.8 17.1 %all-reduce.3 = (f32[128]{0:T(128)S(1)}, f32[128]{0:T(128)S(1)}) all-reduce(f32[128]{0:T(128)S(1)} %bitcast_dynamic-update-slice_fusion.1, f32[128]{0:T(128)S(1)} %bitcast_dynamic-update-slice_fusion.2), channel_id=3, replica_groups=mesh['member'=8,'region'=4] {'member'}, use_global_device_ids=true, to_apply=%add.2 | all-reduce | flops 256 | bytes 2048 | tf_op jit(solution)/shard_map/all_gather | solution.py:59
  69.9 30.5 %all_gather.18 = bf16[512,128]{1,0:T(8,128)(2,1)S(1)} all-gather(bf16[64,128]{1,0:T(8,128)(2,1)S(1)} %bitcast.108), channel_id=1, replica_groups=mesh['member'=8,'region'=4] {'member'}, dimensions={0}, use_global_device_ids=true | all-gather | bytes 147456 | tf_op jit(solution)/shard_map/all_gather | solution.py:56
  101.2 0.7 add_reduce_fusion
  101.8 6.3 %all-reduce.4 = (f32[]{:T(128)}, f32[]{:T(128)}) all-reduce(f32[]{:T(128)} %get-tuple-element.54, f32[]{:T(128)} %get-tuple-element.51), channel_id=1, replica_groups=mesh['member'=8,'region'=4] {'region'}, use_global_device_ids=true, to_apply=%region_3.4 | all-reduce | flops 2 | bytes 16 | tf_op jit(solution)/shard_map/psum | solution.py:65
  109.4 2.0 fusion.29
  111.5 1.0 copy.73
  112.5 4.2 %all-to-all-start = ((bf16[16,4,8192]{2,0,1:T(8,128)(2,1)}), bf16[16,4,8192]{2,0,1:T(8,128)(2,1)}, u32[]{:S(2)}, u32[]{:S(2)}) async-start(bf16[16,4,8192]{2,0,1:T(8,128)(2,1)} %bitcast.95), calls=%async_computation | async-start | bytes 2097152 | tf_op jit(solution)/shard_map/all_to_all | solution.py:40
  117.1 22.7 %psum.31 = f32[512,1]{0,1:T(1,128)S(1)} all-reduce(f32[512,1]{0,1:T(1,128)S(1)} %convolution_bitcast_fusion), channel_id=1, replica_groups=mesh['member'=8,'region'=4] {'region'}, use_global_device_ids=true, to_apply=%region_16.17 | all-reduce | flops 512 | bytes 4096 | tf_op jit(solution)/shard_map/psum | solution.py:68
  139.8 14.4 %all-reduce.7.cloned.1.call-done = f32[512,512]{0,1:T(8,128)} async-done(((f32[512,512]{0,1:T(8,128)}), f32[512,512]{0,1:T(8,128)}) %all-reduce.7.cloned.1.call-update) | async-done | bytes 1048592 | tf_op jit(solution)/shard_map/psum | solution.py:68
  154.2 1.6 convert_add_fusion
  155.8 1.3 copy.54
  157.2 1.4 fusion.4
  158.7 11.7 %cholesky.103 = f32[128,128]{1,0:T(8,128)S(1)} custom-call(f32[128,128]{1,0:T(8,128)S(1)} %cholesky.263), custom_call_target="Cholesky" | custom-call | tf_op jit(solution)/shard_map/jit(cholesky)/cholesky | solution.py:27
  170.4 9.8 %custom-call.34 = f32[1,128,128]{1,2,0:T(8,128)S(1)} custom-call(f32[1,128,128]{2,1,0:T(8,128)S(1)} %get-tuple-element.50), custom_call_target="InvertDiagBlocksLowerTriangular" | custom-call | tf_op jit(solution)/shard_map/jit(cholesky)/cholesky | solution.py:27
  180.9 11.7 %cholesky.215 = f32[128,128]{1,0:T(8,128)S(1)} custom-call(f32[128,128]{1,0:T(8,128)S(1)} %cholesky.267), custom_call_target="Cholesky" | custom-call | tf_op jit(solution)/shard_map/jit(cholesky)/cholesky | solution.py:27
  193.0 10.0 %custom-call.35 = f32[1,128,128]{1,2,0:T(8,128)S(1)} custom-call(f32[1,128,128]{2,1,0:T(8,128)S(1)} %get-tuple-element.48), custom_call_target="InvertDiagBlocksLowerTriangular" | custom-call | tf_op jit(solution)/shard_map/jit(cholesky)/cholesky | solution.py:27
  203.4 1.5 convolution_subtract_fusion.7
  204.9 11.7 %cholesky.236 = f32[128,128]{1,0:T(8,128)S(1)} custom-call(f32[128,128]{1,0:T(8,128)S(1)} %cholesky.272), custom_call_target="Cholesky" | custom-call | tf_op jit(solution)/shard_map/jit(cholesky)/cholesky | solution.py:27
  216.8 9.8 %custom-call.36 = f32[1,128,128]{1,2,0:T(8,128)S(1)} custom-call(f32[1,128,128]{2,1,0:T(8,128)S(1)} %get-tuple-element.46), custom_call_target="InvertDiagBlocksLowerTriangular" | custom-call | tf_op jit(solution)/shard_map/jit(cholesky)/cholesky | solution.py:27
  226.9 1.3 convolution_subtract_fusion.8
  228.3 11.9 %cholesky.253 = f32[128,128]{1,0:T(8,128)S(1)} custom-call(f32[128,128]{1,0:T(8,128)S(1)} %convolution_subtract_fusion.8), custom_call_target="Cholesky" | custom-call | tf_op jit(solution)/shard_map/jit(cholesky)/cholesky | solution.py:27
  240.3 0.7 compare_reduce_fusion.1
  241.0 0.6 compare_reduce_fusion
  241.6 0.7 compare_reduce_fusion.2
  245.0 11.0 %while.1 = (s32[]{:T(128)}, f32[512,512]{0,1:T(8,128)S(1)}, s32[4,2]{0,1:T(2,128)S(1)}, f32[4,128,128]{2,1,0:T(8,128)}, s32[]{:T(128)}) while((s32[]{:T(128)}, f32[512,512]{0,1:T(8,128)S(1)}, s32[4,2]{0,1:T(2,128)S(1)}, f32[4,128,128]{2,1,0:T(8,128)}, s32[]{:T(128)}) %tuple.30), condition=%wide.while_cond, body=%wide.while_body.sunk | while | flops 2 | bytes 393829 | solution.py:29
  245.7 1.3 dynamic-slice.9
  247.1 0.6 bitcast_dynamic-update-slice_fusion.4
  248.4 1.3 dynamic-slice.9
  249.9 0.6 bitcast_dynamic-update-slice_fusion.4
  251.2 1.3 dynamic-slice.9
  253.9 1.3 dynamic-slice.9
  256.0 40.1 %custom-call.37 = f32[4,128,128]{1,2,0:T(8,128)S(1)} custom-call(f32[4,128,128]{2,1,0:T(8,128)} %get-tuple-element.12), custom_call_target="InvertDiagBlocksLowerTriangular" | custom-call | tf_op jit(solution)/shard_map/jit(_cho_solve)/triangular_solve | solution.py:29
  299.1 1.0 convolution_subtract_fusion.5
  300.1 1.8 copy.71
  301.9 1.5 copy.48
  303.5 5.8 %all-to-all-start.1 = ((bf16[64,8,1024]{2,0,1:T(8,128)(2,1)}), bf16[64,8,1024]{2,0,1:T(8,128)(2,1)S(1)}, u32[]{:S(2)}, u32[]{:S(2)}) async-start(bf16[64,8,1024]{2,0,1:T(8,128)(2,1)} %copy.48), calls=%async_computation.1 | async-start | bytes 2097152 | tf_op jit(solution)/shard_map/all_to_all | solution.py:39
  312.8 1.0 convolution_subtract_fusion.4
  314.5 20.2 %all-to-all-done.1 = bf16[64,8,1024]{2,0,1:T(8,128)(2,1)S(1)} async-done(((bf16[64,8,1024]{2,0,1:T(8,128)(2,1)}), bf16[64,8,1024]{2,0,1:T(8,128)(2,1)S(1)}, u32[]{:S(2)}, u32[]{:S(2)}) %all-to-all-start.1) | async-done | bytes 1048608 | tf_op jit(solution)/shard_map/all_to_all | solution.py:39
  335.1 3.7 add_convert_fusion
  338.8 29.1 %all_to_all.79 = bf16[8,64,1024]{2,1,0:T(8,128)(2,1)S(1)} all-to-all(bf16[8,64,1024]{2,1,0:T(8,128)(2,1)S(1)} %bitcast.106), channel_id=1, replica_groups=mesh['member'=8,'region'=4] {'member'}, dimensions={0} | all-to-all | bytes 2097152 | tf_op jit(solution)/shard_map/all_to_all | solution.py:76
  369.0 16.9 %all_to_all.80 = bf16[4,16,8192]{2,1,0:T(8,128)(2,1)S(1)} all-to-all(bf16[4,16,8192]{2,1,0:T(8,128)(2,1)S(1)} %all_to_all.70), channel_id=1, replica_groups=mesh['member'=8,'region'=4] {'region'}, dimensions={0} | all-to-all | bytes 2097152 | tf_op jit(solution)/shard_map/all_to_all | solution.py:75
  385.9 1.0 copy.70
  (91 shorter events, 17.4 us)
Async XLA Ops:
  34.4 16.7 %copy-start.5 = (u32[32]{0:T(128)S(1)}, u32[32]{0:T(128)}, u32[]{:S(2)}) copy-start(u32[32]{0:T(128)} %constant.210) | copy-start | bytes 388
  34.5 18.1 %copy-start.3 = (f32[1,1,16]{2,1,0:T(1,128)S(1)}, f32[1,1,16]{2,1,0:T(1,128)}, u32[]{:S(2)}) copy-start(f32[1,1,16]{2,1,0:T(1,128)} %param.7) | copy-start | bytes 196
  34.5 18.2 %copy-start.4 = (f32[1,1,16]{2,1,0:T(1,128)S(1)}, f32[1,1,16]{2,1,0:T(1,128)}, u32[]{:S(2)}) copy-start(f32[1,1,16]{2,1,0:T(1,128)} %param.6) | copy-start | bytes 196
  41.5 69.9 %copy-start.1 = (bf16[16,32768]{1,0:T(8,128)(2,1)S(1)}, bf16[16,32768]{1,0:T(8,128)(2,1)}, u32[]{:S(2)}) copy-start(bf16[16,32768]{1,0:T(8,128)(2,1)} %param.4) | copy-start | bytes 3145732
  47.9 22.0 %all-to-all-start.2 = ((bf16[16,4,128]{2,0,1:T(8,128)(2,1)}), bf16[16,4,128]{2,0,1:T(8,128)(2,1)S(1)}, u32[]{:S(2)}, u32[]{:S(2)}) async-start(bf16[16,4,128]{2,0,1:T(8,128)(2,1)} %broadcast_select_fusion), calls=%async_computation.2 | async-start | bytes 32768 | tf_op jit(solution)/shard_map/all_to_all | solution.py:54
  51.1 103.1 %all-reduce.7.cloned.1.call-start = ((), (), s32[]{:S(2)}) async-start(), calls=%async_computation.5 | async-start | bytes 2097152 | tf_op jit(solution)/shard_map/psum | solution.py:68
  112.5 187.6 %all-to-all-start = ((bf16[16,4,8192]{2,0,1:T(8,128)(2,1)}), bf16[16,4,8192]{2,0,1:T(8,128)(2,1)}, u32[]{:S(2)}, u32[]{:S(2)}) async-start(bf16[16,4,8192]{2,0,1:T(8,128)(2,1)} %bitcast.95), calls=%async_computation | async-start | bytes 2097152 | tf_op jit(solution)/shard_map/all_to_all | solution.py:40
  154.2 2.9 copy-start
  158.6 34.3 %copy-start.2 = (f32[512,512]{1,0:T(8,128)}, f32[512,512]{1,0:T(8,128)S(1)}, u32[]{:S(2)}) copy-start(f32[512,512]{1,0:T(8,128)S(1)} %fusion.4) | copy-start | bytes 3145732
  303.5 31.2 %all-to-all-start.1 = ((bf16[64,8,1024]{2,0,1:T(8,128)(2,1)}), bf16[64,8,1024]{2,0,1:T(8,128)(2,1)S(1)}, u32[]{:S(2)}, u32[]{:S(2)}) async-start(bf16[64,8,1024]{2,0,1:T(8,128)(2,1)} %copy.48), calls=%async_computation.1 | async-start | bytes 2097152 | tf_op jit(solution)/shard_map/all_to_all | solution.py:39
Sparse Core Ops, SparseCore 0:
  111.6 42.6 all-reduce.6
where the time goes:
time: 399 us; the launch traced here: 394 us
  blocking collectives  150 us (38%)
  other arithmetic  125 us (31%)
  waiting for transfers between devices  34.6 us (9%)
  local copies, waits for them, and re-layouts  33.3 us (8%)
  matrix products  19.1 us (5%)
  between operations  18.9 us (5%)
  starting transfers between devices  13.3 us (3%)
    another operation x14, other arithmetic, mixing_matrix(): factor = jnp.linalg.cholesky(system)  78.8 us
    another operation x3, other arithmetic, mixing_matrix(): solved = jax.scipy.linalg.cho_solve((factor, True), right_side)  40.3 us
    all_gather x1, blocking collectives, local(): obs_rows = lax.all_gather(local_rows, 'member', axis=0, tiled=True)  30.5 us
    all_to_all x1, blocking collectives, local(): lax.all_to_all(updated, 'member', split_axis=0, concat_axis=1, tiled=True)  29.1 us
    psum x1, blocking collectives, local(): products, column = lax.psum((products, column), 'region')  22.7 us
    all_gather x1, blocking collectives, local(): region_offsets = lax.all_gather(obs_offset, 'member', axis=1, tiled=True)  22.5 us
    all_to_all x1, waiting for transfers between devices, local(): lax.all_to_all(lax.all_to_all(ensemble, 'region', split_axis=1, concat_ax...  20.2 us
    all_gather x1, blocking collectives, local(): lax.all_gather(variance, 'member', axis=0, tiled=True)  17.1 us
  transfers between devices with their start and end apart: 4, of which 2 were waited for; matrix products, arithmetic and copies ran while one was open for 38% of the time, Pallas kernels for 0%

commit v1 on v0

v1 whole, which is shorter than its diff:
```python
import functools

import jax
import jax.numpy as jnp
from jax import lax
from jax.experimental import pallas as pl
from jax.experimental.pallas import tpu as pltpu
from jax.sharding import PartitionSpec as P

MESH = pl.DeviceIdType.MESH
F32 = jnp.float32
BF16 = jnp.bfloat16
VMEM_LIMIT = 48 * 1024 * 1024


def peers(members, regions):
    count = members * regions
    own_member, own_region = lax.axis_index("member"), lax.axis_index("region")
    me = own_member * regions + own_region

    def peer(step):
        other = (me + step) % count
        return other, other // regions, other % regions

    return count, me, own_region * members + own_member, peer


def entry_barrier(count, peer):
    barrier = pltpu.get_barrier_semaphore()

    def greet(step, carry):
        _, m, g = peer(step)
        pl.semaphore_signal(barrier, inc=1, device_id=(m, g), device_id_type=MESH)
        return carry

    lax.fori_loop(1, count, greet, 0)
    pl.semaphore_wait(barrier, count - 1)


def gather_kernel(members, regions, ens, off, aux, x_out, picks_out, aux_out, off_all, own_picks,
                  off_send, off_recv, aux_send, aux_recv, x_send, x_recv, pick_send, pick_recv, local_sem):
    count, me, my_block, peer = peers(members, regions)
    links = x_out.shape[2]
    obs = off.shape[0]

    own_off = pltpu.make_async_copy(off, off_all.at[my_block], local_sem.at[0])
    own_aux = pltpu.make_async_copy(aux, aux_out.at[my_block], local_sem.at[1])
    own_x = pltpu.make_async_copy(
        ens.at[:, pl.ds(pl.multiple_of(my_block * links, links), links)], x_out.at[me], local_sem.at[2])
    own_off.start()
    own_aux.start()
    own_x.start()
    entry_barrier(count, peer)

    def off_copy(step, block_at):
        _, m, g = peer(step)
        return pltpu.make_async_remote_copy(
            off, off_all.at[block_at], off_send.at[step], off_recv.at[block_at], (m, g), MESH)

    def aux_copy(step, block_at):
        _, m, g = peer(step)
        return pltpu.make_async_remote_copy(
            aux, aux_out.at[block_at], aux_send.at[step], aux_recv.at[block_at], (m, g), MESH)

    def x_copy(step, row_at):
        _, m, g = peer(step)
        block = g * members + m
        return pltpu.make_async_remote_copy(
            ens.at[:, pl.ds(pl.multiple_of(block * links, links), links)],
            x_out.at[row_at], x_send.at[step], x_recv.at[row_at], (m, g), MESH)

    def pick_copy(step, row_at):
        _, m, g = peer(step)
        return pltpu.make_async_remote_copy(
            own_picks, picks_out.at[row_at], pick_send.at[step], pick_recv.at[row_at], (m, g), MESH)

    def send_small(step, carry):
        off_copy(step, my_block).start()
        return carry

    def send_x(step, carry):
        x_copy(step, me).start()
        aux_copy(step, my_block).start()
        return carry

    def wait_off(step, carry):
        _, m, g = peer(step)
        off_copy(step, g * members + m).wait_recv()
        return carry

    lax.fori_loop(1, count, send_small, 0)
    own_off.wait()
    lax.fori_loop(1, count, wait_off, 0)

    group = 128 // obs

    def pick(chunk, carry):
        parts = []
        for at in range(group):
            block = chunk * group + at
            column = off_all[block][:, :1]
            hot = (lax.broadcasted_iota(jnp.int32, (obs, links), 1) == column).astype(F32).astype(BF16)
            values = ens[:, pl.ds(pl.multiple_of(block * links, links), links)]
            parts.append(lax.dot_general(values, hot, (((1,), (1,)), ((), ())), preferred_element_type=F32))
        own_picks[:, pl.ds(pl.multiple_of(chunk * 128, 128), 128)] = jnp.concatenate(parts, axis=1).astype(BF16)
        return carry

    lax.fori_loop(0, count // group, pick, 0)
    own_pick = pltpu.make_async_copy(own_picks, picks_out.at[me], local_sem.at[3])
    own_pick.start()

    def send_pick(step, carry):
        pick_copy(step, me).start()
        return carry

    lax.fori_loop(1, count, send_pick, 0)
    lax.fori_loop(1, count, send_x, 0)

    def finish(step, carry):
        other, m, g = peer(step)
        block = g * members + m
        pick_copy(step, other).wait()
        aux_copy(step, block).wait()
        x_copy(step, other).wait()
        off_copy(step, block).wait_send()
        return carry

    lax.fori_loop(1, count, finish, 0)
    own_aux.wait()
    own_x.wait()
    own_pick.wait()


def scatter_kernel(members, regions, x, out, send, recv, local_sem):
    count, me, my_block, peer = peers(members, regions)
    links = x.shape[2]

    def columns(block):
        return out.at[:, pl.ds(pl.multiple_of(block * links, links), links)]

    own = pltpu.make_async_copy(x.at[me], columns(my_block), local_sem)
    own.start()
    entry_barrier(count, peer)

    def copy(step, block_at):
        other, m, g = peer(step)
        return pltpu.make_async_remote_copy(
            x.at[other], columns(block_at), send.at[step], recv.at[block_at], (m, g), MESH)

    def start(step, carry):
        copy(step, my_block).start()
        return carry

    def finish(step, carry):
        _, m, g = peer(step)
        copy(step, g * members + m).wait()
        return carry

    lax.fori_loop(1, count, start, 0)
    lax.fori_loop(1, count, finish, 0)
    own.wait()


def halves(value):
    high = value.astype(BF16)
    return high, (value - high.astype(F32)).astype(BF16)


def mix_kernel(picks, values, variance, x, out, a_f, a_h, a_l, w_f, w_h, w_l, z_f):
    size = picks.shape[0]
    width = min(256, size)
    dot = functools.partial(jnp.dot, preferred_element_type=F32)
    exact = functools.partial(jnp.dot, preferred_element_type=F32, precision=lax.Precision.HIGHEST)

    def each(total, body):
        def step(chunk, carry):
            body(pl.ds(pl.multiple_of(chunk * width, width), width), chunk * width)
            return carry

        lax.fori_loop(0, total // width, step, 0)

    def eye(start, columns):
        rows = lax.broadcasted_iota(jnp.int32, (size, columns), 0)
        return (rows == lax.broadcasted_iota(jnp.int32, (size, columns), 1) + start).astype(F32)

    picked = picks[...].astype(F32)
    center = jnp.sum(picked, axis=0, keepdims=True) / size
    anomaly = picked - center
    innovation = values[...] - center
    spread = jnp.sum(anomaly * anomaly, axis=0, keepdims=True) / (size - 1.0) + variance[...]
    lift = jnp.sum(innovation * innovation, axis=1, keepdims=True) / jnp.sum(spread, axis=1, keepdims=True)
    inflation = jnp.sqrt(lift)
    weight = 1.0 / ((size - 1.0) * variance[...])
    column = jnp.sum(anomaly * (lift * weight * innovation), axis=1, keepdims=True)
    scaled = anomaly * jnp.sqrt(lift * weight)
    flipped = scaled.T
    for start in range(0, size, width):
        chunk = slice(start, start + width)
        a_f[:, chunk] = exact(scaled, flipped[:, chunk]) + eye(start, width)
    a_h[...], a_l[...] = halves(a_f[...])

    def square(cols, start):
        z_f[:, cols] = (
            dot(a_h[...], a_h[:, cols]) + dot(a_l[...], a_h[:, cols]) + dot(a_h[...], a_l[:, cols])
        )

    each(size, square)
    norm = jnp.max(jnp.sum(jnp.abs(z_f[:, :size]), axis=1, keepdims=True))
    plain = jnp.max(jnp.sum(jnp.abs(a_f[...]), axis=1, keepdims=True))
    top = jnp.minimum(jnp.sqrt(norm) * 1.01, plain * 1.0001)
    gentle = top < 400.0

    def opening(square_of):
        start = 2.0 / (1.0 + top)
        ratio = (top - 1.0) / (top + 1.0)
        scale = 2.0 / (2.0 - ratio * ratio)
        w_f[:, :size] = scale * (2.0 * start * a_f[...] - start * start * square_of)
        w_f[:, size:] = scale * start * (2.0 * eye(0, size) - start * a_f[...])
        return ratio * ratio / (2.0 - ratio * ratio)

    def refine(product, tolerance, limit, bound):
        def going(state):
            return jnp.logical_and(state[0] > tolerance, state[1] < limit)

        def step(state):
            bound, count = state
            scale = 2.0 / (2.0 - bound * bound)
            product(scale)
            w_f[...] = z_f[...]
            return bound * bound / (2.0 - bound * bound), count + 1

        lax.while_loop(going, step, (bound, 0))

    @pl.when(gentle)
    def _():
        bound = opening(z_f[:, :size])

        def product(scale):
            w_h[...], w_l[...] = halves(w_f[...])

            def body(cols, start):
                z_f[:, cols] = scale * (2.0 * w_f[:, cols] - (
                    dot(w_h[:, :size], w_h[:, cols]) + dot(w_l[:, :size], w_h[:, cols]) + dot(w_h[:, :size], w_l[:, cols])
                ))

            each(2 * size, body)

        refine(product, 0.01, 24, bound)
        w_h[:, size:], w_l[:, size:] = halves(w_f[:, size:])

        def residual(cols, start):
            right = pl.ds(pl.multiple_of(size + start, width), width)
            w_h[:, cols] = (eye(start, width) - (
                dot(a_h[...], w_h[:, right]) + dot(a_l[...], w_h[:, right]) + dot(a_h[...], w_l[:, right])
            )).astype(BF16)

        def correct(cols, start):
            right = pl.ds(pl.multiple_of(size + start, width), width)
            z_f[:, cols] = w_f[:, right] + dot(w_h[:, size:], w_h[:, cols])

        each(size, residual)
        each(size, correct)

    @pl.when(jnp.logical_not(gentle))
    def _():
        def square_exact(cols, start):
            z_f[:, cols] = exact(a_f[...], a_f[:, cols])

        each(size, square_exact)
        bound = opening(z_f[:, :size])

        def product(scale):
            def body(cols, start):
                z_f[:, cols] = scale * (2.0 * w_f[:, cols] - exact(w_f[:, :size], w_f[:, cols]))

            each(2 * size, body)

        refine(product, 0.01, 40, bound)

        def again(count, carry):
            def residual(cols, start):
                right = pl.ds(pl.multiple_of(size + start, width), width)
                w_f[:, cols] = eye(start, width) - exact(a_f[...], w_f[:, right])

            def correct(cols, start):
                right = pl.ds(pl.multiple_of(size + start, width), width)
                z_f[:, cols] = w_f[:, right] + exact(w_f[:, size:], w_f[:, cols])

            each(size, residual)
            each(size, correct)
            w_f[:, size:] = z_f[:, :size]
            return carry

        lax.fori_loop(0, 2, again, 0)

    inverse = z_f[:, :size]
    gain = jnp.sum(inverse * column, axis=0, keepdims=True)
    mixing = 0.5 * inflation * (eye(0, size) + inverse) + (gain + (1.0 - inflation) / size)
    a_h[...], a_l[...] = halves(mixing)

    def apply(cols, start):
        out[:, cols] = (dot(a_h[...], x[:, cols]) + dot(a_l[...], x[:, cols])).astype(BF16)

    each(x.shape[1], apply)


def local(ensemble, obs_offset, observed, obs_var):
    members = lax.axis_size("member")
    regions = lax.axis_size("region")
    count = members * regions
    own = ensemble.shape[0]
    size = own * count
    links = ensemble.shape[1] // count
    obs = obs_offset.shape[2]
    total = count * obs
    offsets = jnp.broadcast_to(obs_offset.reshape(obs, 1), (obs, 128))
    aux = jnp.zeros((8, 128), F32).at[0, :obs].set(observed.reshape(-1)).at[1, :obs].set(obs_var.reshape(-1))
    vmem = pl.BlockSpec(memory_space=pltpu.VMEM)
    sems = pltpu.SemaphoreType.DMA((count,))
    x, picks, every_aux = pl.pallas_call(
        functools.partial(gather_kernel, members, regions),
        out_shape=(
            jax.ShapeDtypeStruct((count, own, links), BF16),
            jax.ShapeDtypeStruct((count, own, total), BF16),
            jax.ShapeDtypeStruct((count, 8, 128), F32),
        ),
        in_specs=[vmem] * 3,
        out_specs=(vmem,) * 3,
        scratch_shapes=[
            pltpu.VMEM((count, obs, 128), jnp.int32),
            pltpu.VMEM((own, total), BF16),
        ] + [sems] * 8 + [pltpu.SemaphoreType.DMA((4,))],
        compiler_params=pltpu.CompilerParams(
            collective_id=0, has_side_effects=True, vmem_limit_bytes=VMEM_LIMIT),
    )(ensemble, offsets, aux)
    values = every_aux[:, 0, :obs].reshape(1, total)
    variance = every_aux[:, 1, :obs].reshape(1, total)
    mixed = pl.pallas_call(
        mix_kernel,
        out_shape=jax.ShapeDtypeStruct((size, links), BF16),
        in_specs=[vmem] * 4,
        out_specs=vmem,
        scratch_shapes=[
            pltpu.VMEM((size, size), F32),
            pltpu.VMEM((size, size), BF16),
            pltpu.VMEM((size, size), BF16),
            pltpu.VMEM((size, 2 * size), F32),
            pltpu.VMEM((size, 2 * size), BF16),
            pltpu.VMEM((size, 2 * size), BF16),
            pltpu.VMEM((size, 2 * size), F32),
        ],
        compiler_params=pltpu.CompilerParams(vmem_limit_bytes=VMEM_LIMIT),
    )(picks.reshape(size, total), values, variance, x.reshape(size, links))
    return pl.pallas_call(
        functools.partial(scatter_kernel, members, regions),
        out_shape=jax.ShapeDtypeStruct(ensemble.shape, BF16),
        in_specs=[vmem],
        out_specs=vmem,
        scratch_shapes=[sems, sems, pltpu.SemaphoreType.DMA],
        compiler_params=pltpu.CompilerParams(
            collective_id=1, has_side_effects=True, vmem_limit_bytes=VMEM_LIMIT),
    )(mixed.reshape(count, own, links))


def solution(mesh):
    return jax.shard_map(
        local,
        mesh=mesh,
        in_specs=(
            P(("member", "region"), None),
            P("region", "member", None),
            P("region", "member", None),
            P("region", "member", None),
        ),
        out_specs=P(("member", "region"), None),
        check_vma=False,
    )
```

time: 399 us -> 134 us (0.34)
  the two profiles are of different devices: /device:TPU:0 before, /device:TPU:15 now
where the time goes in v1:
time: 134 us
  Pallas kernels  130 us (97%)
  local copies, waits for them, and re-layouts  4.47 us (3%)
    pallas_call x1, Pallas kernels, local(): pl.pallas_call(functools.partial(gather_kernel, members, regions), out_sh...  54.5 us
    pallas_call x1, Pallas kernels, local(): pl.pallas_call(mix_kernel, out_shape=jax.ShapeDtypeStruct((size, links),...  44.4 us
    pallas_call x1, Pallas kernels, local(): pl.pallas_call(functools.partial(scatter_kernel, members, regions), out_s...  30.9 us
    unnamed x9, local copies, waits for them, and re-layouts  4.07 us

profile of v1, /device:TPU:15, one launch (start us, length us, event | category | flops | bytes accessed | tf_op | source)
XLA Modules:
  0.0 134.2 jit_solution(6643204030080970146)
XLA Ops:
  0.0 0.0 copy-start.1
  0.0 0.7 copy-done.1
  0.7 0.0 copy-start.3
  0.7 0.6 copy-done.3
  1.3 0.0 copy-start.2
  1.3 0.1 scatter.9.aux
  1.4 0.6 copy-done.2
  2.0 0.1 broadcast_in_dim.9.off
  2.0 0.0 copy-start
  2.0 1.2 copy-done
  3.3 54.5 %shard_map.46 = (bf16[32,16,1024]{2,1,0:T(8,128)(2,1)S(1)}, bf16[32,16,512]{2,1,0:T(8,128)(2,1)S(1)}, f32[32,8,128]{2,1,0:T(8,128)S(1)}) custom-call(bf16[16,32768]{1,0:T(8,128)(2,1)S(1)} %copy-done, s32[16,128]{1,0:T(8,128)S(1)} %broadcast_in_dim.9.off, f32[8,128]{1,0:T(8,128)S(1)} %scatter.9.aux), custom_call_target="tpu_custom_call" | custom-call | tf_op jit(solution)/shard_map/pallas_call | solution.py:320
  57.7 0.1 slice_reduce_fusion
  57.8 0.1 reshape_squeeze.7.variance
  57.9 0.1 reshape_squeeze.6.values
  58.0 44.4 %shard_map.47 = bf16[512,1024]{1,0:T(8,128)(2,1)S(1)} custom-call(bf16[512,512]{1,0:T(8,128)(2,1)S(1)} %bitcast.8, f32[1,512]{1,0:T(1,128)S(1)} %reshape_squeeze.6.values, f32[1,512]{1,0:T(1,128)S(1)} %reshape_squeeze.7.variance, bf16[512,1024]{1,0:T(8,128)(2,1)S(1)} %bitcast.7), custom_call_target="tpu_custom_call" | custom-call | tf_op jit(solution)/shard_map/pallas_call | solution.py:338
  102.4 30.9 %shard_map.48 = bf16[16,32768]{1,0:T(8,128)(2,1)S(1)} custom-call(bf16[32,16,1024]{2,1,0:T(8,128)(2,1)S(1)} %bitcast.6), custom_call_target="tpu_custom_call" | custom-call | tf_op jit(solution)/shard_map/pallas_call | solution.py:354
  133.2 1.0 copy.7
  (1 shorter events, 0.0 us)
Async XLA Ops:
  0.0 0.7 copy-start.1
  0.7 0.7 copy-start.3
  1.3 0.7 copy-start.2
  2.0 1.2 copy-start

commit v2 on v1

v2 whole, which is shorter than its diff:
```python
import functools

import jax
import jax.numpy as jnp
from jax import lax
from jax.experimental import pallas as pl
from jax.experimental.pallas import tpu as pltpu
from jax.sharding import PartitionSpec as P

MESH = pl.DeviceIdType.MESH
F32 = jnp.float32
BF16 = jnp.bfloat16
VMEM_LIMIT = 56 * 1024 * 1024


def peers(members, regions):
    count = members * regions
    own_member, own_region = lax.axis_index("member"), lax.axis_index("region")
    me = own_member * regions + own_region

    def peer(step):
        other = (me + step) % count
        return other, other // regions, other % regions

    return count, me, own_region * members + own_member, peer


def entry_barrier(count, peer):
    barrier = pltpu.get_barrier_semaphore()

    def greet(step, carry):
        _, m, g = peer(step)
        pl.semaphore_signal(barrier, inc=1, device_id=(m, g), device_id_type=MESH)
        return carry

    lax.fori_loop(1, count, greet, 0)
    pl.semaphore_wait(barrier, count - 1)


def halves(value):
    high = value.astype(BF16)
    return high, (value - high.astype(F32)).astype(BF16)


def eye(size, start, columns):
    rows = lax.broadcasted_iota(jnp.int32, (size, columns), 0)
    return (rows == lax.broadcasted_iota(jnp.int32, (size, columns), 1) + start).astype(F32)


def each(total, width, body):
    def step(chunk, carry):
        body(pl.ds(pl.multiple_of(chunk * width, width), width), chunk * width)
        return carry

    lax.fori_loop(0, total // width, step, 0)


dot = functools.partial(jnp.dot, preferred_element_type=F32)
exact = functools.partial(jnp.dot, preferred_element_type=F32, precision=lax.Precision.HIGHEST)


def dot_nt(left, right):
    return lax.dot_general(left, right, (((1,), (1,)), ((), ())), preferred_element_type=F32)


def spectrum_bound(squared, plain):
    norm = jnp.max(jnp.sum(jnp.abs(squared), axis=1, keepdims=True), axis=0, keepdims=True)
    other = jnp.max(jnp.sum(jnp.abs(plain), axis=1, keepdims=True), axis=0, keepdims=True)
    return jnp.minimum(jnp.sqrt(norm) * 1.01, other * 1.0001)


def opening(size, top, a_f, squared, w_f):
    start = 2.0 / (1.0 + top)
    ratio = (top - 1.0) / (top + 1.0)
    scale = 2.0 / (2.0 - ratio * ratio)
    w_f[:, :size] = scale * (2.0 * start * a_f[...] - start * start * squared)
    w_f[:, size:] = scale * start * (2.0 * eye(size, 0, size) - start * a_f[...])
    return ratio * ratio / (2.0 - ratio * ratio)


def gather_kernel(members, regions, ens, off, aux, x_out, a_f, inv, col, scal, off_all, aux_all, own_picks, picks,
                  rows, s_h, s_l, a_h, a_l, w_f, w_h, w_l,
                  off_send, off_recv, aux_send, aux_recv, x_send, x_recv, one_send, one_recv, two_send, two_recv,
                  local_sem):
    count, me, my_block, peer = peers(members, regions)
    my_m, my_g = lax.axis_index("member"), lax.axis_index("region")
    links = x_out.shape[2]
    obs = off.shape[0]
    total = own_picks.shape[1]
    size = a_f.shape[0]
    width = min(256, size)
    group = 128 // obs

    own_off = pltpu.make_async_copy(off, off_all.at[my_block], local_sem.at[0])
    own_aux = pltpu.make_async_copy(aux, aux_all.at[my_block], local_sem.at[1])
    own_x = pltpu.make_async_copy(
        ens.at[:, pl.ds(pl.multiple_of(my_block * links, links), links)], x_out.at[me], local_sem.at[2])
    own_off.start()
    own_aux.start()
    own_x.start()
    entry_barrier(count, peer)

    def off_copy(step, block_at):
        _, m, g = peer(step)
        return pltpu.make_async_remote_copy(
            off, off_all.at[block_at], off_send.at[step], off_recv.at[block_at], (m, g), MESH)

    def aux_copy(step, block_at):
        _, m, g = peer(step)
        return pltpu.make_async_remote_copy(
            aux, aux_all.at[block_at], aux_send.at[step], aux_recv.at[block_at], (m, g), MESH)

    def x_copy(m, g, row_at):
        block = g * members + m
        return pltpu.make_async_remote_copy(
            ens.at[:, pl.ds(pl.multiple_of(block * links, links), links)],
            x_out.at[row_at], x_send.at[m * regions + g], x_recv.at[row_at], (m, g), MESH)

    def one_copy(m, m_at):
        return pltpu.make_async_remote_copy(
            own_picks, picks.at[m_at, my_g], one_send.at[m], one_recv.at[m_at], (m, my_g), MESH)

    def two_copy(g, g_at):
        return pltpu.make_async_remote_copy(
            picks.at[:, my_g], picks.at[:, g_at], two_send.at[g], two_recv.at[g_at], (my_m, g), MESH)

    def loop(low, high, body):
        def step(at, carry):
            body(at)
            return carry

        lax.fori_loop(low, high, step, 0)

    def next_m(step):
        return (my_m + step) % members

    def next_g(step):
        return (my_g + step) % regions

    loop(1, count, lambda step: off_copy(step, my_block).start())
    loop(1, count, lambda step: aux_copy(step, my_block).start())
    loop(1, members, lambda step: x_copy(next_m(step), my_g, me).start())
    own_off.wait()

    def wait_off(step):
        _, m, g = peer(step)
        off_copy(step, g * members + m).wait_recv()

    loop(1, count, wait_off)

    def pick(chunk):
        parts = []
        for at in range(group):
            block = chunk * group + at
            column = off_all[block][:, :1]
            hot = (lax.broadcasted_iota(jnp.int32, (obs, links), 1) == column).astype(F32).astype(BF16)
            values = ens[:, pl.ds(pl.multiple_of(block * links, links), links)]
            parts.append(dot_nt(values, hot))
        own_picks[:, pl.ds(pl.multiple_of(chunk * 128, 128), 128)] = jnp.concatenate(parts, axis=1).astype(BF16)

    loop(0, count // group, pick)
    own_pick = pltpu.make_async_copy(own_picks, picks.at[my_m, my_g], local_sem.at[3])
    own_pick.start()
    loop(1, members, lambda step: one_copy(next_m(step), my_m).start())
    own_pick.wait()
    loop(1, members, lambda step: one_copy(next_m(step), next_m(step)).wait_recv())
    loop(1, regions, lambda step: two_copy(next_g(step), my_g).start())

    def send_rest(step):
        x_copy((my_m + step // (regions - 1)) % members, next_g(1 + step % (regions - 1)), me).start()

    loop(0, members * (regions - 1), send_rest)
    own_aux.wait()

    def wait_aux(step):
        _, m, g = peer(step)
        aux_copy(step, g * members + m).wait_recv()

    loop(1, count, wait_aux)
    lane = lax.broadcasted_iota(jnp.int32, (8, 128), 1) // obs

    def spread_aux(chunk):
        value = jnp.zeros((8, 128), F32)
        for at in range(group):
            value = jnp.where(lane == at, aux_all[chunk * group + at], value)
        rows[:, pl.ds(pl.multiple_of(chunk * 128, 128), 128)] = value

    loop(0, count // group, spread_aux)
    loop(1, regions, lambda step: two_copy(next_g(step), next_g(step)).wait_recv())

    values, variance = rows[0:1, :], rows[1:2, :]
    picked = picks[...].astype(F32).reshape(size, total)
    center = jnp.sum(picked, axis=0, keepdims=True) / size
    anomaly = picked - center
    innovation = values - center
    spread = jnp.sum(anomaly * anomaly, axis=0, keepdims=True) / (size - 1.0) + variance
    lift = jnp.sum(innovation * innovation, axis=1, keepdims=True) / jnp.sum(spread, axis=1, keepdims=True)
    weight = 1.0 / ((size - 1.0) * variance)
    column = jnp.sum(anomaly * (lift * weight * innovation), axis=1, keepdims=True)
    col[...] = jnp.broadcast_to(column, col.shape)
    s_h[...], s_l[...] = halves(anomaly * jnp.sqrt(lift * weight))

    def products(cols, start):
        a_f[:, cols] = eye(size, start, width) + (
            dot_nt(s_h[...], s_h[cols, :]) + dot_nt(s_l[...], s_h[cols, :]) + dot_nt(s_h[...], s_l[cols, :])
        )

    each(size, width, products)
    a_h[...], a_l[...] = halves(a_f[...])

    def square(cols, start):
        inv[:, cols] = (
            dot(a_h[...], a_h[:, cols]) + dot(a_l[...], a_h[:, cols]) + dot(a_h[...], a_l[:, cols])
        )

    each(size, width, square)
    top = spectrum_bound(inv[...], a_f[...])
    scal[...] = jnp.where(lax.broadcasted_iota(jnp.int32, scal.shape, 0) == 0, lift, top)
    bound = opening(size, top, a_f, inv[...], w_f)

    def full_step(count, bound):
        scale = 2.0 / (2.0 - bound * bound)
        w_h[...], w_l[...] = halves(w_f[...])

        def body(cols, start):
            w_f[:, cols] = scale * (2.0 * w_f[:, cols] - (
                dot(w_h[:, :size], w_h[:, cols]) + dot(w_l[:, :size], w_h[:, cols]) + dot(w_h[:, :size], w_l[:, cols])
            ))

        each(2 * size, width, body)
        return bound * bound / (2.0 - bound * bound)

    bound = lax.fori_loop(0, 3, full_step, bound)
    scale = 2.0 / (2.0 - bound * bound)
    w_h[...] = w_f[...].astype(BF16)

    def last_step(cols, start):
        right = pl.ds(pl.multiple_of(size + start, width), width)
        w_f[:, right] = scale * (2.0 * w_f[:, right] - dot(w_h[:, :size], w_h[:, right]))

    each(size, width, last_step)
    w_h[:, size:], w_l[:, size:] = halves(w_f[:, size:])

    def correct(cols, start):
        right = pl.ds(pl.multiple_of(size + start, width), width)
        rest = eye(size, start, width) - (
            dot(a_h[...], w_h[:, right]) + dot(a_l[...], w_h[:, right]) + dot(a_h[...], w_l[:, right])
        )
        inv[:, cols] = w_f[:, right] + dot(w_h[:, size:], rest.astype(BF16))

    each(size, width, correct)

    def finish_all(step):
        off_copy(step, my_block).wait_send()
        aux_copy(step, my_block).wait_send()
        other, m, g = peer(step)
        x_copy(m, g, other).wait()

    loop(1, count, finish_all)
    loop(1, members, lambda step: one_copy(next_m(step), my_m).wait_send())
    loop(1, regions, lambda step: two_copy(next_g(step), my_g).wait_send())
    own_x.wait()


def scatter_kernel(members, regions, x, out, send, recv, local_sem):
    count, me, my_block, peer = peers(members, regions)
    links = x.shape[2]

    def columns(block):
        return out.at[:, pl.ds(pl.multiple_of(block * links, links), links)]

    own = pltpu.make_async_copy(x.at[me], columns(my_block), local_sem)
    own.start()
    entry_barrier(count, peer)

    def copy(step, block_at):
        other, m, g = peer(step)
        return pltpu.make_async_remote_copy(
            x.at[other], columns(block_at), send.at[step], recv.at[block_at], (m, g), MESH)

    def start(step, carry):
        copy(step, my_block).start()
        return carry

    def finish(step, carry):
        _, m, g = peer(step)
        copy(step, g * members + m).wait()
        return carry

    lax.fori_loop(1, count, start, 0)
    lax.fori_loop(1, count, finish, 0)
    own.wait()


def mix_kernel(col, scal, inv, x, a_any, out, a_f, m_h, m_l, w_f, z_f, sem):
    size = inv.shape[0]
    width = min(256, size)
    lift = scal[0:1, 0:1]
    inflation = jnp.sqrt(lift)
    column = col[:, :1]

    def finish(inverse):
        gain = jnp.sum(inverse * column, axis=0, keepdims=True)
        m_h[...], m_l[...] = halves(
            0.5 * inflation * (eye(size, 0, size) + inverse) + (gain + (1.0 - inflation) / size))

    gentle = jnp.max(scal[1:2, :]) < 150.0

    @pl.when(gentle)
    def _():
        finish(inv[...])

    @pl.when(jnp.logical_not(gentle))
    def _():
        fetch = pltpu.make_async_copy(a_any, a_f, sem)
        fetch.start()
        fetch.wait()

        def square_exact(cols, start):
            z_f[:, cols] = exact(a_f[...], a_f[:, cols])

        each(size, width, square_exact)
        top = jnp.max(spectrum_bound(z_f[:, :size], a_f[...]))
        bound = opening(size, top, a_f, z_f[:, :size], w_f)

        def going(state):
            return jnp.logical_and(state[0] > 0.01, state[1] < 40)

        def step(state):
            bound, count = state
            scale = 2.0 / (2.0 - bound * bound)

            def body(cols, start):
                z_f[:, cols] = scale * (2.0 * w_f[:, cols] - exact(w_f[:, :size], w_f[:, cols]))

            each(2 * size, width, body)
            w_f[...] = z_f[...]
            return bound * bound / (2.0 - bound * bound), count + 1

        lax.while_loop(going, step, (bound, 0))

        def again(count, carry):
            def residual(cols, start):
                right = pl.ds(pl.multiple_of(size + start, width), width)
                w_f[:, cols] = eye(size, start, width) - exact(a_f[...], w_f[:, right])

            def correct(cols, start):
                right = pl.ds(pl.multiple_of(size + start, width), width)
                z_f[:, cols] = w_f[:, right] + exact(w_f[:, size:], w_f[:, cols])

            each(size, width, residual)
            each(size, width, correct)
            w_f[:, size:] = z_f[:, :size]
            return carry

        lax.fori_loop(0, 2, again, 0)
        finish(z_f[:, :size])

    def apply(cols, start):
        out[:, cols] = (dot(m_h[...], x[:, cols]) + dot(m_l[...], x[:, cols])).astype(BF16)

    each(x.shape[1], width, apply)


def local(ensemble, obs_offset, observed, obs_var):
    members = lax.axis_size("member")
    regions = lax.axis_size("region")
    count = members * regions
    own = ensemble.shape[0]
    size = own * count
    links = ensemble.shape[1] // count
    obs = obs_offset.shape[2]
    total = count * obs
    offsets = jnp.broadcast_to(obs_offset.reshape(obs, 1), (obs, 128))
    aux = jnp.tile(jnp.concatenate([observed.reshape(1, obs), obs_var.reshape(1, obs)], axis=0), (4, 128 // obs))
    vmem = pl.BlockSpec(memory_space=pltpu.VMEM)
    sems = pltpu.SemaphoreType.DMA((count,))
    member_sems = pltpu.SemaphoreType.DMA((members,))
    region_sems = pltpu.SemaphoreType.DMA((regions,))
    x, system, inverse, column, scalars = pl.pallas_call(
        functools.partial(gather_kernel, members, regions),
        out_shape=(
            jax.ShapeDtypeStruct((count, own, links), BF16),
            jax.ShapeDtypeStruct((size, size), F32),
            jax.ShapeDtypeStruct((size, size), F32),
            jax.ShapeDtypeStruct((size, 128), F32),
            jax.ShapeDtypeStruct((8, 128), F32),
        ),
        in_specs=[vmem] * 3,
        out_specs=(vmem,) * 5,
        scratch_shapes=[
            pltpu.VMEM((count, obs, 128), jnp.int32),
            pltpu.VMEM((count, 8, 128), F32),
            pltpu.VMEM((own, total), BF16),
            pltpu.VMEM((members, regions, own, total), BF16),
            pltpu.VMEM((8, total), F32),
            pltpu.VMEM((size, total), BF16),
            pltpu.VMEM((size, total), BF16),
            pltpu.VMEM((size, size), BF16),
            pltpu.VMEM((size, size), BF16),
            pltpu.VMEM((size, 2 * size), F32),
            pltpu.VMEM((size, 2 * size), BF16),
            pltpu.VMEM((size, 2 * size), BF16),
        ] + [sems] * 6 + [member_sems] * 2 + [region_sems] * 2 + [pltpu.SemaphoreType.DMA((4,))],
        compiler_params=pltpu.CompilerParams(
            collective_id=0, has_side_effects=True, vmem_limit_bytes=VMEM_LIMIT),
    )(ensemble, offsets, aux)
    mixed = pl.pallas_call(
        mix_kernel,
        out_shape=jax.ShapeDtypeStruct((size, links), BF16),
        in_specs=[vmem] * 4 + [pl.BlockSpec(memory_space=pl.ANY)],
        out_specs=vmem,
        scratch_shapes=[
            pltpu.VMEM((size, size), F32),
            pltpu.VMEM((size, size), BF16),
            pltpu.VMEM((size, size), BF16),
            pltpu.VMEM((size, 2 * size), F32),
            pltpu.VMEM((size, 2 * size), F32),
            pltpu.SemaphoreType.DMA,
        ],
        compiler_params=pltpu.CompilerParams(vmem_limit_bytes=VMEM_LIMIT),
    )(column, scalars, inverse, x.reshape(size, links), system)
    return pl.pallas_call(
        functools.partial(scatter_kernel, members, regions),
        out_shape=jax.ShapeDtypeStruct(ensemble.shape, BF16),
        in_specs=[vmem],
        out_specs=vmem,
        scratch_shapes=[sems, sems, pltpu.SemaphoreType.DMA],
        compiler_params=pltpu.CompilerParams(
            collective_id=1, has_side_effects=True, vmem_limit_bytes=VMEM_LIMIT),
    )(mixed.reshape(count, own, links))


def solution(mesh):
    return jax.shard_map(
        local,
        mesh=mesh,
        in_specs=(
            P(("member", "region"), None),
            P("region", "member", None),
            P("region", "member", None),
            P("region", "member", None),
        ),
        out_specs=P(("member", "region"), None),
        check_vma=False,
    )
```

time: 134 us -> 141 us (1.052)
  Pallas kernels: 130 us -> 135 us
    pallas_call x1, Pallas kernels: 54.5 us -> 57.5 us  [local(): pl.pallas_call(functools.partial(gather_kernel, members, regions), out_sh...]
    pallas_call x1, Pallas kernels: 30.9 us -> 32.9 us  [local(): pl.pallas_call(functools.partial(scatter_kernel, members, regions), out_s...]
    unnamed x9 -> x7, local copies, waits for them, and re-layouts: 4.07 us -> 3.58 us
where the time goes in v2:
time: 141 us; the launch traced here: 140 us
  Pallas kernels  135 us (96%)
  local copies, waits for them, and re-layouts  4.91 us (3%)
    pallas_call x1, Pallas kernels, local(): pl.pallas_call(functools.partial(gather_kernel, members, regions), out_sh...  57.5 us
    pallas_call x1, Pallas kernels, local(): pl.pallas_call(mix_kernel, out_shape=jax.ShapeDtypeStruct((size, links),...  45.1 us
    pallas_call x1, Pallas kernels, local(): pl.pallas_call(functools.partial(scatter_kernel, members, regions), out_s...  32.9 us
    unnamed x7, local copies, waits for them, and re-layouts  3.58 us

profile of v2, /device:TPU:15, one launch (start us, length us, event | category | flops | bytes accessed | tf_op | source)
XLA Modules:
  0.0 140.4 jit_solution(7324115510272633498)
XLA Ops:
  0.0 0.0 copy-start.1
  0.0 0.0 copy-start.2
  0.0 0.7 copy-done.1
  0.7 0.0 copy-done.2
  0.7 0.0 copy-start
  0.7 0.6 copy-done
  1.3 0.7 broadcast_in_dim.8.off
  2.0 0.7 tile.10.aux
  2.7 57.5 %shard_map.46 = (bf16[32,16,1024]{2,1,0:T(8,128)(2,1)}, f32[512,512]{1,0:T(8,128)}, f32[512,512]{1,0:T(8,128)}, f32[512,128]{1,0:T(8,128)}, f32[8,128]{1,0:T(8,128)}) custom-call(bf16[16,32768]{1,0:T(8,128)(2,1)} %ens.1, s32[16,128]{1,0:T(8,128)} %broadcast_in_dim.8.off, f32[8,128]{1,0:T(8,128)} %tile.10.aux), custom_call_target="tpu_custom_call" | custom-call | tf_op jit(solution)/shard_map/pallas_call | solution.py:380
  60.1 45.1 %shard_map.47 = bf16[512,1024]{1,0:T(8,128)(2,1)} custom-call(f32[512,128]{1,0:T(8,128)} %get-tuple-element.10.col, f32[8,128]{1,0:T(8,128)} %get-tuple-element.11.scal, f32[512,512]{1,0:T(8,128)} %get-tuple-element.12.inv, bf16[512,1024]{1,0:T(8,128)(2,1)} %bitcast.8, f32[512,512]{1,0:T(8,128)} %get-tuple-element.14.a_any), custom_call_target="tpu_custom_call" | custom-call | tf_op jit(solution)/shard_map/pallas_call | solution.py:408
  105.2 32.9 %shard_map.48 = bf16[16,32768]{1,0:T(8,128)(2,1)} custom-call(bf16[32,16,1024]{2,1,0:T(8,128)(2,1)} %bitcast.7), custom_call_target="tpu_custom_call" | custom-call | tf_op jit(solution)/shard_map/pallas_call | solution.py:423
  138.1 2.3 %copy.6 = bf16[16,32768]{1,0:T(8,128)(2,1)} copy(bf16[16,32768]{1,0:T(8,128)(2,1)} %shard_map.48) | data formatting | bytes 2097152
  (2 shorter events, 0.0 us)
Async XLA Ops:
  0.0 0.7 copy-start.1
  0.0 0.7 copy-start.2
  0.7 0.7 copy-start

commit v3 on v2

--- a/solution.py
+++ b/solution.py
@@ -10,7 +10,7 @@
 MESH = pl.DeviceIdType.MESH
 F32 = jnp.float32
 BF16 = jnp.bfloat16
-VMEM_LIMIT = 56 * 1024 * 1024
+MIB = 1024 * 1024
 
 
 def peers(members, regions):
@@ -139,7 +139,6 @@
 
     loop(1, count, lambda step: off_copy(step, my_block).start())
     loop(1, count, lambda step: aux_copy(step, my_block).start())
-    loop(1, members, lambda step: x_copy(next_m(step), my_g, me).start())
     own_off.wait()
 
     def wait_off(step):
@@ -162,6 +161,7 @@
     own_pick = pltpu.make_async_copy(own_picks, picks.at[my_m, my_g], local_sem.at[3])
     own_pick.start()
     loop(1, members, lambda step: one_copy(next_m(step), my_m).start())
+    loop(1, members, lambda step: x_copy(next_m(step), my_g, me).start())
     own_pick.wait()
     loop(1, members, lambda step: one_copy(next_m(step), next_m(step)).wait_recv())
     loop(1, regions, lambda step: two_copy(next_g(step), my_g).start())
@@ -403,7 +403,7 @@
             pltpu.VMEM((size, 2 * size), BF16),
         ] + [sems] * 6 + [member_sems] * 2 + [region_sems] * 2 + [pltpu.SemaphoreType.DMA((4,))],
         compiler_params=pltpu.CompilerParams(
-            collective_id=0, has_side_effects=True, vmem_limit_bytes=VMEM_LIMIT),
+            collective_id=0, has_side_effects=True, vmem_limit_bytes=min(56, 20 + total // 64) * MIB),
     )(ensemble, offsets, aux)
     mixed = pl.pallas_call(
         mix_kernel,
@@ -418,7 +418,7 @@
             pltpu.VMEM((size, 2 * size), F32),
             pltpu.SemaphoreType.DMA,
         ],
-        compiler_params=pltpu.CompilerParams(vmem_limit_bytes=VMEM_LIMIT),
+        compiler_params=pltpu.CompilerParams(vmem_limit_bytes=24 * MIB),
     )(column, scalars, inverse, x.reshape(size, links), system)
     return pl.pallas_call(
         functools.partial(scatter_kernel, members, regions),
@@ -427,7 +427,7 @@
         out_specs=vmem,
         scratch_shapes=[sems, sems, pltpu.SemaphoreType.DMA],
         compiler_params=pltpu.CompilerParams(
-            collective_id=1, has_side_effects=True, vmem_limit_bytes=VMEM_LIMIT),
+            collective_id=1, has_side_effects=True, vmem_limit_bytes=12 * MIB),
     )(mixed.reshape(count, own, links))
 
 

time: 141 us -> 128 us (0.908)
  Pallas kernels: 135 us -> 124 us
    pallas_call x1, Pallas kernels: 57.5 us -> 50.5 us  [local(): pl.pallas_call(functools.partial(gather_kernel, members, regions), out_sh...]
    pallas_call x1, Pallas kernels: 45.1 us -> 41.3 us  [local(): pl.pallas_call(mix_kernel, out_shape=jax.ShapeDtypeStruct((size, links),...]
    unnamed x7 -> x9, local copies, waits for them, and re-layouts: 3.58 us -> 3.51 us
where the time goes in v3:
time: 128 us; the launch traced here: 127 us
  Pallas kernels  124 us (97%)
  local copies, waits for them, and re-layouts  3.66 us (3%)
    pallas_call x1, Pallas kernels, local(): pl.pallas_call(functools.partial(gather_kernel, members, regions), out_sh...  50.5 us
    pallas_call x1, Pallas kernels, local(): pl.pallas_call(mix_kernel, out_shape=jax.ShapeDtypeStruct((size, links),...  41.3 us
    pallas_call x1, Pallas kernels, local(): pl.pallas_call(functools.partial(scatter_kernel, members, regions), out_s...  31.9 us
    unnamed x9, local copies, waits for them, and re-layouts  3.51 us

profile of v3, /device:TPU:15, one launch (start us, length us, event | category | flops | bytes accessed | tf_op | source)
XLA Modules:
  0.0 127.4 jit_solution(10140624235612709998)
XLA Ops:
  0.0 0.0 copy-start.2
  0.0 0.0 copy-start.3
  0.0 0.7 copy-done.2
  0.7 0.0 copy-done.3
  0.7 0.0 copy-start.1
  0.7 0.6 copy-done.1
  1.3 0.1 broadcast_in_dim.8.off
  1.4 0.1 tile.10.aux
  1.5 0.0 copy-start
  1.5 1.2 copy-done
  2.7 50.5 %shard_map.46 = (bf16[32,16,1024]{2,1,0:T(8,128)(2,1)S(1)}, f32[512,512]{1,0:T(8,128)S(1)}, f32[512,512]{1,0:T(8,128)S(1)}, f32[512,128]{1,0:T(8,128)S(1)}, f32[8,128]{1,0:T(8,128)S(1)}) custom-call(bf16[16,32768]{1,0:T(8,128)(2,1)S(1)} %copy-done, s32[16,128]{1,0:T(8,128)S(1)} %broadcast_in_dim.8.off, f32[8,128]{1,0:T(8,128)S(1)} %tile.10.aux), custom_call_target="tpu_custom_call" | custom-call | tf_op jit(solution)/shard_map/pallas_call | solution.py:380
  53.2 41.3 %shard_map.47 = bf16[512,1024]{1,0:T(8,128)(2,1)S(1)} custom-call(f32[512,128]{1,0:T(8,128)S(1)} %get-tuple-element.10.col, f32[8,128]{1,0:T(8,128)S(1)} %get-tuple-element.11.scal, f32[512,512]{1,0:T(8,128)S(1)} %get-tuple-element.12.inv, bf16[512,1024]{1,0:T(8,128)(2,1)S(1)} %bitcast.8, f32[512,512]{1,0:T(8,128)S(1)} %get-tuple-element.14.a_any), custom_call_target="tpu_custom_call" | custom-call | tf_op jit(solution)/shard_map/pallas_call | solution.py:408
  94.6 31.9 %shard_map.48 = bf16[16,32768]{1,0:T(8,128)(2,1)S(1)} custom-call(bf16[32,16,1024]{2,1,0:T(8,128)(2,1)S(1)} %bitcast.7), custom_call_target="tpu_custom_call" | custom-call | tf_op jit(solution)/shard_map/pallas_call | solution.py:423
  126.5 1.0 copy.6
  (2 shorter events, 0.0 us)
Async XLA Ops:
  0.0 0.7 copy-start.2
  0.0 0.7 copy-start.3
  0.7 0.7 copy-start.1
  1.5 1.2 copy-start

commit v4 on v3

--- a/solution.py
+++ b/solution.py
@@ -78,7 +78,7 @@
     return ratio * ratio / (2.0 - ratio * ratio)
 
 
-def gather_kernel(members, regions, ens, off, aux, x_out, a_f, inv, col, scal, off_all, aux_all, own_picks, picks,
+def gather_kernel(members, regions, source, off, aux, x_out, a_f, inv, col, scal, ens, off_all, aux_all, own_picks, picks,
                   rows, s_h, s_l, a_h, a_l, w_f, w_h, w_l,
                   off_send, off_recv, aux_send, aux_recv, x_send, x_recv, one_send, one_recv, two_send, two_recv,
                   local_sem):
@@ -95,9 +95,10 @@
     own_aux = pltpu.make_async_copy(aux, aux_all.at[my_block], local_sem.at[1])
     own_x = pltpu.make_async_copy(
         ens.at[:, pl.ds(pl.multiple_of(my_block * links, links), links)], x_out.at[me], local_sem.at[2])
+    fetch = pltpu.make_async_copy(source, ens, local_sem.at[4])
+    fetch.start()
     own_off.start()
     own_aux.start()
-    own_x.start()
     entry_barrier(count, peer)
 
     def off_copy(step, block_at):
@@ -146,6 +147,8 @@
         off_copy(step, g * members + m).wait_recv()
 
     loop(1, count, wait_off)
+    fetch.wait()
+    own_x.start()
 
     def pick(chunk):
         parts = []
@@ -230,7 +233,15 @@
         each(2 * size, width, body)
         return bound * bound / (2.0 - bound * bound)
 
-    bound = lax.fori_loop(0, 3, full_step, bound)
+    bound = lax.fori_loop(0, 2, full_step, bound)
+    third = 2.0 / (2.0 - bound * bound)
+    w_h[...] = w_f[...].astype(BF16)
+
+    def third_step(cols, start):
+        w_f[:, cols] = third * (2.0 * w_f[:, cols] - dot(w_h[:, :size], w_h[:, cols]))
+
+    each(2 * size, width, third_step)
+    bound = bound * bound / (2.0 - bound * bound)
     scale = 2.0 / (2.0 - bound * bound)
     w_h[...] = w_f[...].astype(BF16)
 
@@ -386,9 +397,10 @@
             jax.ShapeDtypeStruct((size, 128), F32),
             jax.ShapeDtypeStruct((8, 128), F32),
         ),
-        in_specs=[vmem] * 3,
+        in_specs=[pl.BlockSpec(memory_space=pltpu.HBM), vmem, vmem],
         out_specs=(vmem,) * 5,
         scratch_shapes=[
+            pltpu.VMEM(ensemble.shape, BF16),
             pltpu.VMEM((count, obs, 128), jnp.int32),
             pltpu.VMEM((count, 8, 128), F32),
             pltpu.VMEM((own, total), BF16),
@@ -401,7 +413,7 @@
             pltpu.VMEM((size, 2 * size), F32),
             pltpu.VMEM((size, 2 * size), BF16),
             pltpu.VMEM((size, 2 * size), BF16),
-        ] + [sems] * 6 + [member_sems] * 2 + [region_sems] * 2 + [pltpu.SemaphoreType.DMA((4,))],
+        ] + [sems] * 6 + [member_sems] * 2 + [region_sems] * 2 + [pltpu.SemaphoreType.DMA((5,))],
         compiler_params=pltpu.CompilerParams(
             collective_id=0, has_side_effects=True, vmem_limit_bytes=min(56, 20 + total // 64) * MIB),
     )(ensemble, offsets, aux)

time: 128 us -> 126 us (0.984)
  no operation moved by 1% of the time
where the time goes in v4:
time: 126 us
  Pallas kernels  123 us (98%)
  local copies, waits for them, and re-layouts  3.66 us (3%)
    pallas_call x1, Pallas kernels, local(): pl.pallas_call(functools.partial(gather_kernel, members, regions), out_sh...  49.3 us
    pallas_call x1, Pallas kernels, local(): pl.pallas_call(mix_kernel, out_shape=jax.ShapeDtypeStruct((size, links),...  41.3 us
    pallas_call x1, Pallas kernels, local(): pl.pallas_call(functools.partial(scatter_kernel, members, regions), out_s...  31.9 us
    unnamed x9, local copies, waits for them, and re-layouts  3.51 us

profile of v4, /device:TPU:15, one launch (start us, length us, event | category | flops | bytes accessed | tf_op | source)
XLA Modules:
  0.0 126.3 jit_solution(4992455693387538241)
XLA Ops:
  0.0 0.0 copy-start.2
  0.0 0.0 copy-start.3
  0.0 0.7 copy-done.2
  0.7 0.0 copy-done.3
  0.7 0.0 copy-start.1
  0.7 0.6 copy-done.1
  1.3 0.1 broadcast_in_dim.8.off
  1.4 0.1 tile.10.aux
  1.5 0.0 copy-start
  1.5 1.2 copy-done
  2.7 49.3 %shard_map.46 = (bf16[32,16,1024]{2,1,0:T(8,128)(2,1)S(1)}, f32[512,512]{1,0:T(8,128)S(1)}, f32[512,512]{1,0:T(8,128)S(1)}, f32[512,128]{1,0:T(8,128)S(1)}, f32[8,128]{1,0:T(8,128)S(1)}) custom-call(bf16[16,32768]{1,0:T(8,128)(2,1)S(1)} %copy-done, s32[16,128]{1,0:T(8,128)S(1)} %broadcast_in_dim.8.off, f32[8,128]{1,0:T(8,128)S(1)} %tile.10.aux), custom_call_target="tpu_custom_call" | custom-call | tf_op jit(solution)/shard_map/pallas_call | solution.py:391
  52.0 41.3 %shard_map.47 = bf16[512,1024]{1,0:T(8,128)(2,1)S(1)} custom-call(f32[512,128]{1,0:T(8,128)S(1)} %get-tuple-element.10.col, f32[8,128]{1,0:T(8,128)S(1)} %get-tuple-element.11.scal, f32[512,512]{1,0:T(8,128)S(1)} %get-tuple-element.12.inv, bf16[512,1024]{1,0:T(8,128)(2,1)S(1)} %bitcast.8, f32[512,512]{1,0:T(8,128)S(1)} %get-tuple-element.14.a_any), custom_call_target="tpu_custom_call" | custom-call | tf_op jit(solution)/shard_map/pallas_call | solution.py:420
  93.4 31.9 %shard_map.48 = bf16[16,32768]{1,0:T(8,128)(2,1)S(1)} custom-call(bf16[32,16,1024]{2,1,0:T(8,128)(2,1)S(1)} %bitcast.7), custom_call_target="tpu_custom_call" | custom-call | tf_op jit(solution)/shard_map/pallas_call | solution.py:435
  125.3 1.0 copy.6
  (2 shorter events, 0.0 us)
Async XLA Ops:
  0.0 0.7 copy-start.2
  0.0 0.7 copy-start.3
  0.7 0.7 copy-start.1
  1.5 1.2 copy-start
